TPU v7x, 128 devices: a whole 4x4x4 slice. The times are simulated.
128 devices in a mesh: row: 16 (over z, y_hi, core), col: 8 (over y_lo, x).
Axes of the slice: x: 4, y: 4 (y_hi: 2, y_lo: 2; y = y_hi * 2 + y_lo), z: 4, core: 2. Of those that a mesh axis runs over, the one named last changes fastest.
Arguments:
- velocity: float32 [3, 128, 128, 128], P(None, 'row', 'col'), may hold values from -6 to 6
Outputs:
- advanced: float32 [3, 128, 128, 128], P(None, 'row', 'col')
All inputs are finite; a program needn't handle non-finite values.
Results may differ from a plain program's by a relative error of at most 0.0003.
Values sent between devices are 32-bit elements.
A program may use at most 64 MiB of HBM per device.

v0:
```python
import functools

import jax
import jax.numpy as jnp
import numpy as np
from jax import lax
from jax.experimental import pallas as pl
from jax.experimental.pallas import tpu as pltpu
from jax.sharding import PartitionSpec as P

N = 128
BAND = 43
KEPT = 85
PAD = 96
HALF = 64
F32 = jnp.float32
BF16 = jnp.bfloat16
VMEM = pltpu.VMEM
STEP = 2.0 / N


def split_np(table):
    high = table.astype(np.float32).astype(BF16)
    low = (table - high.astype(np.float64)).astype(np.float32).astype(BF16)
    return high, low


def tables():
    turn = 2.0 * np.pi / N
    cell = np.arange(N)
    kz = np.arange(BAND)
    angle_z = turn * ((cell[:, None] * kz[None, :]) % N)
    z_forward = np.zeros((N, N))
    z_forward[:, :BAND] = np.cos(angle_z) / N
    z_forward[:, HALF : HALF + BAND] = -np.sin(angle_z) / N
    weight = np.where(kz == 0, 1.0, 2.0)
    z_inverse = np.zeros((N, N))
    z_inverse[:BAND] = (np.cos(angle_z) * weight).T
    z_inverse[HALF : HALF + BAND] = (-np.sin(angle_z) * weight).T
    z_turned = np.concatenate([z_inverse[HALF:], -z_inverse[:HALF]])
    z_pair = np.concatenate([z_inverse, z_turned])
    wave = np.arange(KEPT)
    wave = np.where(wave < BAND, wave, wave - KEPT)
    angle = turn * ((wave[:, None] * cell[None, :]) % N)
    forward = np.zeros((2 * PAD, N))
    forward[:KEPT] = np.cos(angle) / N
    forward[PAD : PAD + KEPT] = np.sin(angle) / N
    inverse = np.zeros((2 * N, PAD))
    inverse[:N, :KEPT] = np.cos(angle).T
    inverse[N:, :KEPT] = np.sin(angle).T

    def left(table):
        high, low = split_np(table)
        return np.concatenate([high, high, low], axis=1)

    def right(table):
        high, low = split_np(table)
        return np.concatenate([high, high, low], axis=0)

    return right(z_forward), right(z_inverse), right(z_pair), left(forward), left(inverse)


def halves(value):
    high = value.astype(BF16)
    low = (value - high.astype(F32)).astype(BF16)
    return high, low


def times(value, table):
    high, low = halves(value)
    return jnp.dot(
        jnp.concatenate([high, low, high], axis=1), table, preferred_element_type=F32
    )


def under(table, value):
    high, low = halves(value)
    return jnp.dot(
        table, jnp.concatenate([high, low, high], axis=0), preferred_element_type=F32
    )


def column_of(row, col):
    chip = (row // 2) * 8 + col
    spare = jnp.where((chip % 3 == 0) & (chip < 63), 64 + chip // 3, 4096)
    return jnp.where(row % 2 == 1, chip, spare)


def holder_of(column):
    chip = jnp.where(column < 64, column, (column - 64) * 3)
    core = jnp.where(column < 64, 1, 0)
    return (chip // 8) * 2 + core, chip % 8


def kernel(
    v_hbm, zf_hbm, zi_hbm, zp_hbm, xf_hbm, xi_hbm, o_hbm,
    vin, zf, zi, zp, xf, xi, s0, r0, fs, fr, is6, ir6, is3, ir3, t0, q0, out, a0, acc,
    load_sem, store_sem, ready_sem, row_s, row_r, fwd_s, fwd_r, inv_s, inv_r,
):
    row, col = lax.axis_index("row"), lax.axis_index("col")
    me = col * 16 + row
    ki = column_of(row, col)
    active = ki < KEPT
    idle = jnp.logical_not(active)

    loads = [
        pltpu.make_async_copy(src, dst, load_sem.at[n])
        for n, (src, dst) in enumerate(
            [(v_hbm, vin), (zf_hbm, zf), (xf_hbm, xf), (xi_hbm, xi), (zp_hbm, zp), (zi_hbm, zi)]
        )
    ]
    for load in loads:
        load.start()

    barrier = pltpu.get_barrier_semaphore()
    for j in range(1, 16):
        pl.semaphore_signal(barrier, inc=1, device_id=((row + j) % 16, col))
    for j in range(1, 8):
        pl.semaphore_signal(barrier, inc=1, device_id=(row, (col + j) % 8))

    lane = lax.broadcasted_iota(jnp.int32, (1, N), 1)
    side = jnp.where(lane < HALF, 1.0, -1.0).astype(F32)

    def turned(value):
        return pltpu.roll(value, HALF, 1) * side

    def part(value, c):
        return value[:, c * N : (c + 1) * N]

    def fold(both, rows, sign):
        outs = []
        for c in range(both.shape[1] // N):
            piece = part(both, c)
            outs.append(piece[:rows] + sign * turned(piece[rows:]))
        return outs

    def x_forward(parts):
        return fold(under(xf[...], jnp.concatenate(parts, axis=1)), PAD, 1.0)

    def x_inverse_pair(parts):
        return under(xi[...], jnp.concatenate(parts, axis=1))

    def row_exchange(src, dst, slot):
        for j in range(1, 16):
            to = (row + j) % 16
            pltpu.make_async_remote_copy(
                src.at[to], dst.at[row], row_s.at[slot], row_r.at[slot], device_id=(to, col)
            ).start()
        dst[row] = src[row]
        pltpu.make_async_copy(
            dst.at[pl.ds(0, 15)], dst.at[pl.ds(0, 15)], row_r.at[slot]
        ).wait()

    def copy_rows(src, at, dst, to, rows):
        for n in range(rows):
            dst[pl.ds(to * rows + n, 1), :] = src[pl.ds(at * rows + n, 1), :]

    def wait_rows(ref, count, sem):
        pltpu.make_async_copy(ref.at[pl.ds(0, count)], ref.at[pl.ds(0, count)], sem).wait()

    def send_forward(p):
        def body(j, carry):
            i = j + jnp.where(j >= ki, 1, 0)
            pltpu.make_async_remote_copy(
                fs.at[p, pl.ds(i * 3, 3)], fr.at[p, pl.ds(me * 3, 3)],
                fwd_s.at[p], fwd_r.at[p], device_id=holder_of(i),
            ).start()
            return carry

        lax.fori_loop(0, jnp.where(active, KEPT - 1, KEPT), body, 0)

    def put_forward(p, parts):
        for c in range(3):
            fs[p, pl.ds(c, PAD, stride=3), :] = parts[c]

    def take_forward(p):
        copy_rows(fs.at[p], ki, fr.at[p], me, 3)
        wait_rows(fr.at[p], 127 * 3, fwd_r.at[p])
        return [fr[p, pl.ds(c, N, stride=3), :] for c in range(3)]

    def send_inverse(src, dst, p, rows):
        def body(j, carry):
            d = j + jnp.where(j >= me, 1, 0)
            pltpu.make_async_remote_copy(
                src.at[pl.ds(d * rows, rows)], dst.at[pl.ds(ki * rows, rows)],
                inv_s.at[p], inv_r.at[p], device_id=(d % 16, d // 16),
            ).start()
            return carry

        lax.fori_loop(0, 127, body, 0)

    def take_inverse(src, dst, p, rows):
        @pl.when(active)
        def _():
            copy_rows(src, me, dst, ki, rows)
            wait_rows(dst, (KEPT - 1) * rows, inv_r.at[p])

        @pl.when(idle)
        def _():
            wait_rows(dst, KEPT * rows, inv_r.at[p])

        return [dst[pl.ds(c, PAD, stride=rows), :] for c in range(rows)]

    kx = jnp.where(ki < BAND, ki, ki - KEPT).astype(F32)
    ky_at = lax.broadcasted_iota(jnp.int32, (PAD, N), 0)
    ky = jnp.where(ky_at < BAND, ky_at, ky_at - KEPT).astype(F32)
    kz = (lax.broadcasted_iota(jnp.int32, (PAD, N), 1) % HALF).astype(F32)

    def norm():
        return kx * kx + ky * ky + kz * kz

    def spectral(p):
        b = x_forward(take_forward(p))
        squared = norm()
        along = (kx * b[0] + ky * b[1] + kz * b[2]) / jnp.where(squared > 0, squared, 1.0)
        return [b[0] - kx * along, b[1] - ky * along, b[2] - kz * along]

    def scatter(state, ref, rows):
        outs = fold(x_inverse_pair(state), N, -1.0)
        for c in range(rows):
            ref[pl.ds(c, N, stride=rows), :] = outs[c]

    def with_curl(a):
        cross = [
            ky * a[2] - kz * a[1],
            kz * a[0] - kx * a[2],
            kx * a[1] - ky * a[0],
        ]
        return list(a) + [-turned(w) for w in cross]

    loads[0].wait()
    loads[1].wait()
    lines = times(vin[...], zf[...])
    for n in range(24):
        s0[:, n, :] = lines[n * 16 : (n + 1) * 16]
    for p in range(2):
        ir6[p, pl.ds(KEPT * 6, (PAD - KEPT) * 6), :] = jnp.zeros(((PAD - KEPT) * 6, N), F32)
    ir3[pl.ds(KEPT * 3, (PAD - KEPT) * 3), :] = jnp.zeros(((PAD - KEPT) * 3, N), F32)

    pl.semaphore_wait(barrier, 22)
    for j in range(1, 8):
        pl.semaphore_signal(ready_sem, inc=1, device_id=(row, (col + j) % 8))
    row_exchange(s0, r0, 0)
    loads[2].wait()
    put_forward(0, x_forward([r0[:, c * 8 : (c + 1) * 8, :].reshape(N, N) for c in range(3)]))
    pl.semaphore_wait(ready_sem, 7)
    send_forward(0)
    for load in loads[3:]:
        load.wait()

    @pl.when(active)
    def _():
        a = spectral(0)
        for c in range(3):
            a0[c] = a[c]
        scatter(with_curl(a), is6.at[0], 6)
        send_inverse(is6.at[0], ir6.at[0], 0, 6)

    for p in range(2):
        got = take_inverse(is6.at[p], ir6.at[p], p, 6)
        both = x_inverse_pair(got)
        grids = []
        for c in range(6):
            piece = part(both, c)
            grids.append(times(jnp.concatenate([piece[:N], piece[N:]], axis=1), zp[...]))
        u, w = grids[:3], grids[3:]
        product = [
            u[1] * w[2] - u[2] * w[1],
            u[2] * w[0] - u[0] * w[2],
            u[0] * w[1] - u[1] * w[0],
        ]
        put_forward(p + 1, x_forward([times(n, zf[...]) for n in product]))
        send_forward(p + 1)

        @pl.when(active)
        def _():
            b = spectral(p + 1)
            damp = norm() * (1.0 / N)
            if p == 0:
                nxt = []
                for c in range(3):
                    base = a0[c]
                    rate = b[c] - damp * base
                    acc[c] = base + (0.5 * STEP) * rate
                    nxt.append(base + STEP * rate)
                    a0[c] = nxt[c]
                scatter(with_curl(nxt), is6.at[1], 6)
                send_inverse(is6.at[1], ir6.at[1], 1, 6)
            else:
                last = []
                for c in range(3):
                    last.append(acc[c] + (0.5 * STEP) * (b[c] - damp * a0[c]))
                scatter(last, is3, 3)
                send_inverse(is3, ir3, 2, 3)

    got = take_inverse(is3, ir3, 2, 3)
    ends = fold(x_inverse_pair(got), N, -1.0)
    for c in range(3):
        t0[:, c * 8 : (c + 1) * 8, :] = ends[c].reshape(16, 8, N)
    row_exchange(t0, q0, 1)
    final = times(q0[...].reshape(384, N), zi[...])
    for y in range(16):
        for c in range(3):
            at = y * 24 + c * 8
            out[pl.ds(c * 128 + y, 8, stride=16), :] = final[at : at + 8]
    store = pltpu.make_async_copy(out, o_hbm, store_sem)
    store.start()

    for slot in range(2):
        pltpu.make_async_copy(s0.at[pl.ds(0, 15)], s0.at[pl.ds(0, 15)], row_s.at[slot]).wait()
    for p in range(3):
        @pl.when(active)
        def _():
            wait_rows(fs.at[p], (KEPT - 1) * 3, fwd_s.at[p])
            if p < 2:
                wait_rows(is6.at[p], 127 * 6, inv_s.at[p])
            else:
                wait_rows(is3, 127 * 3, inv_s.at[p])

        @pl.when(idle)
        def _():
            wait_rows(fs.at[p], KEPT * 3, fwd_s.at[p])

    store.wait()


def local(velocity):
    consts = tables()
    shapes = [((384, N), F32)] + [(t.shape, BF16) for t in consts]
    scratch = [VMEM(shape, kind) for shape, kind in shapes]
    scratch += [
        VMEM((16, 24, N), F32), VMEM((16, 24, N), F32),
        VMEM((3, PAD * 3, N), F32), VMEM((3, N * 3, N), F32),
        VMEM((2, N * 6, N), F32), VMEM((2, PAD * 6, N), F32),
        VMEM((N * 3, N), F32), VMEM((PAD * 3, N), F32),
        VMEM((16, 24, N), F32), VMEM((16, 24, N), F32),
        VMEM((384, N), F32), VMEM((3, PAD, N), F32), VMEM((3, PAD, N), F32),
        pltpu.SemaphoreType.DMA((6,)), pltpu.SemaphoreType.DMA(()),
        pltpu.SemaphoreType.REGULAR,
        pltpu.SemaphoreType.DMA((2,)), pltpu.SemaphoreType.DMA((2,)),
        pltpu.SemaphoreType.DMA((3,)), pltpu.SemaphoreType.DMA((3,)),
        pltpu.SemaphoreType.DMA((3,)), pltpu.SemaphoreType.DMA((3,)),
    ]
    anywhere = pl.BlockSpec(memory_space=pl.ANY)
    result = pl.pallas_call(
        kernel,
        out_shape=jax.ShapeDtypeStruct((384, N), F32),
        in_specs=[anywhere] * 6,
        out_specs=anywhere,
        scratch_shapes=scratch,
        compiler_params=pltpu.CompilerParams(collective_id=0, has_side_effects=True),
        name="heun",
    )(velocity.reshape(384, N), *[jnp.asarray(t) for t in consts])
    return result.reshape(3, 8, 16, N)


def solution(mesh):
    placed = (P(None, "row", "col", None),)
    return jax.shard_map(
        local, mesh=mesh, in_specs=placed, out_specs=P(None, "row", "col", None), check_vma=False
    )
```

profile of v0, /device:TPU:1, one launch (start us, length us, event | category | flops | bytes accessed | tf_op | source)
XLA Modules:
  0.0 73.1 jit_solution(6963895692356888703)
XLA Ops:
  0.0 71.5 %heun.1 = f32[384,128]{1,0:T(8,128)} custom-call(f32[384,128]{1,0:T(8,128)} %bitcast.3, bf16[384,128]{1,0:T(8,128)(2,1)} %constant.10.clone.zf_hbm, bf16[384,128]{1,0:T(8,128)(2,1)} %constant.11.clone.zi_hbm, bf16[768,128]{1,0:T(8,128)(2,1)} %constant.12.clone.zp_hbm, bf16[192,384]{1,0:T(8,128)(2,1)} %constant.13.clone.xf_hbm, ...), custom_call_target="tpu_custom_call" | custom-call | tf_op jit(solution)/shard_map/heun/pallas_call | solution.py:345
  71.5 1.6 %copy.8 = f32[3,8,16,128]{3,2,1,0:T(8,128)} copy(f32[3,8,16,128]{3,2,1,0:T(8,128)} %bitcast.2) | data formatting | bytes 393216
where the time goes:
time: 73.6 us; the launch traced here: 73.1 us
  Pallas kernels  71.5 us (97%)
  local copies, waits for them, and re-layouts  1.62 us (2%)
    pallas_call x1, Pallas kernels, local(): pl.pallas_call(kernel, out_shape=jax.ShapeDtypeStruct((384, N), F32), in_...  71.5 us
    unnamed x1, local copies, waits for them, and re-layouts  1.62 us

commit v1 on v0

--- a/solution.py
+++ b/solution.py
@@ -1,4 +1,4 @@
-import functools
+import itertools
 
 import jax
 import jax.numpy as jnp
@@ -17,6 +17,11 @@
 BF16 = jnp.bfloat16
 VMEM = pltpu.VMEM
 STEP = 2.0 / N
+MOVES = sorted(
+    itertools.product(range(4), repeat=3), key=lambda move: -sum((0, 1, 2, 1)[d] for d in move)
+)
+ROW_MOVES = [move for move in itertools.product(range(4), range(2), range(2)) if any(move)]
+ROW_MOVES.sort(key=lambda move: -((0, 1, 2, 1)[move[0]] + 2 * move[1]))
 
 
 def split_np(table):
@@ -86,12 +91,6 @@
     return jnp.where(row % 2 == 1, chip, spare)
 
 
-def holder_of(column):
-    chip = jnp.where(column < 64, column, (column - 64) * 3)
-    core = jnp.where(column < 64, 1, 0)
-    return (chip // 8) * 2 + core, chip % 8
-
-
 def kernel(
     v_hbm, zf_hbm, zi_hbm, zp_hbm, xf_hbm, xi_hbm, o_hbm,
     vin, zf, zi, zp, xf, xi, s0, r0, fs, fr, is6, ir6, is3, ir3, t0, q0, out, a0, acc,
@@ -118,6 +117,7 @@
     for j in range(1, 8):
         pl.semaphore_signal(barrier, inc=1, device_id=(row, (col + j) % 8))
 
+    z_at, y_at, x_at, core = row // 4, (row // 2 % 2) * 2 + col // 4, col % 4, row % 2
     lane = lax.broadcasted_iota(jnp.int32, (1, N), 1)
     side = jnp.where(lane < HALF, 1.0, -1.0).astype(F32)
 
@@ -141,8 +141,12 @@
         return under(xi[...], jnp.concatenate(parts, axis=1))
 
     def row_exchange(src, dst, slot):
-        for j in range(1, 16):
-            to = (row + j) % 16
+        for move in ROW_MOVES:
+            to = (
+                (z_at + move[0]) % 4 * 4
+                + (row // 2 + move[1]) % 2 * 2
+                + (core + move[2]) % 2
+            )
             pltpu.make_async_remote_copy(
                 src.at[to], dst.at[row], row_s.at[slot], row_r.at[slot], device_id=(to, col)
             ).start()
@@ -158,16 +162,33 @@
     def wait_rows(ref, count, sem):
         pltpu.make_async_copy(ref.at[pl.ds(0, count)], ref.at[pl.ds(0, count)], sem).wait()
 
+    def chip_at(move):
+        z, y, x = (z_at + move[0]) % 4, (y_at + move[1]) % 4, (x_at + move[2]) % 4
+        return z * 4 + (y // 2) * 2, (y % 2) * 4 + x
+
     def send_forward(p):
-        def body(j, carry):
-            i = j + jnp.where(j >= ki, 1, 0)
+        def one(i, to):
             pltpu.make_async_remote_copy(
                 fs.at[p, pl.ds(i * 3, 3)], fr.at[p, pl.ds(me * 3, 3)],
-                fwd_s.at[p], fwd_r.at[p], device_id=holder_of(i),
+                fwd_s.at[p], fwd_r.at[p], device_id=to,
             ).start()
-            return carry
-
-        lax.fori_loop(0, jnp.where(active, KEPT - 1, KEPT), body, 0)
+
+        for move in MOVES:
+            base, side_col = chip_at(move)
+            chip = (base // 2) * 8 + side_col
+            spare = (chip % 3 == 0) & (chip < 63)
+            near = move == (0, 0, 0)
+
+            @pl.when(spare & (core == 1) if near else spare)
+            def _():
+                one(64 + chip // 3, (base, side_col))
+
+            if near:
+                @pl.when(core == 0)
+                def _():
+                    one(chip, (base + 1, side_col))
+            else:
+                one(chip, (base + 1, side_col))
 
     def put_forward(p, parts):
         for c in range(3):
@@ -179,15 +200,18 @@
         return [fr[p, pl.ds(c, N, stride=3), :] for c in range(3)]
 
     def send_inverse(src, dst, p, rows):
-        def body(j, carry):
-            d = j + jnp.where(j >= me, 1, 0)
+        def one(to):
+            d = to[1] * 16 + to[0]
             pltpu.make_async_remote_copy(
                 src.at[pl.ds(d * rows, rows)], dst.at[pl.ds(ki * rows, rows)],
-                inv_s.at[p], inv_r.at[p], device_id=(d % 16, d // 16),
+                inv_s.at[p], inv_r.at[p], device_id=to,
             ).start()
-            return carry
-
-        lax.fori_loop(0, 127, body, 0)
+
+        for move in MOVES:
+            base, side_col = chip_at(move)
+            for other in range(2):
+                if move != (0, 0, 0) or other:
+                    one((base + (core + other) % 2, side_col))
 
     def take_inverse(src, dst, p, rows):
         @pl.when(active)

time: 73.6 us -> 67.1 us (0.912)
  Pallas kernels: 71.5 us -> 65.4 us
    pallas_call x1, Pallas kernels: 71.5 us -> 65.4 us  [local(): pl.pallas_call(kernel, out_shape=jax.ShapeDtypeStruct((384, N), F32), in_...]
where the time goes in v1:
time: 67.1 us; the launch traced here: 67 us
  Pallas kernels  65.4 us (97%)
  local copies, waits for them, and re-layouts  1.62 us (2%)
    pallas_call x1, Pallas kernels, local(): pl.pallas_call(kernel, out_shape=jax.ShapeDtypeStruct((384, N), F32), in_...  65.4 us
    unnamed x1, local copies, waits for them, and re-layouts  1.62 us

profile of v1, /device:TPU:1, one launch (start us, length us, event | category | flops | bytes accessed | tf_op | source)
XLA Modules:
  0.0 67.0 jit_solution(4289151750730814919)
XLA Ops:
  0.0 65.4 %heun.1 = f32[384,128]{1,0:T(8,128)} custom-call(f32[384,128]{1,0:T(8,128)} %bitcast.3, bf16[384,128]{1,0:T(8,128)(2,1)} %constant.10.clone.zf_hbm, bf16[384,128]{1,0:T(8,128)(2,1)} %constant.11.clone.zi_hbm, bf16[768,128]{1,0:T(8,128)(2,1)} %constant.12.clone.zp_hbm, bf16[192,384]{1,0:T(8,128)(2,1)} %constant.13.clone.xf_hbm, ...), custom_call_target="tpu_custom_call" | custom-call | tf_op jit(solution)/shard_map/heun/pallas_call | solution.py:369
  65.4 1.6 %copy.8 = f32[3,8,16,128]{3,2,1,0:T(8,128)} copy(f32[3,8,16,128]{3,2,1,0:T(8,128)} %bitcast.2) | data formatting | bytes 393216

commit v2 on v1

--- a/solution.py
+++ b/solution.py
@@ -43,7 +43,24 @@
     z_inverse[:BAND] = (np.cos(angle_z) * weight).T
     z_inverse[HALF : HALF + BAND] = (-np.sin(angle_z) * weight).T
     z_turned = np.concatenate([z_inverse[HALF:], -z_inverse[:HALF]])
-    z_pair = np.concatenate([z_inverse, z_turned])
+
+    def spares(first, count):
+        lanes = np.arange(count) + BAND
+        waves = np.arange(count) + first
+        return np.concatenate([lanes, lanes + HALF]), np.concatenate([waves, waves + HALF])
+
+    z_third = np.zeros((2, N, N))
+    z_third_back = np.zeros((2, N, N))
+    for r in range(2):
+        lanes, waves = spares(1 + 21 * r, 21)
+        z_third[r][:, lanes] = z_forward[:, waves]
+        z_third_back[r][lanes] = z_inverse[waves]
+    z_third[0][:, HALF] = z_forward[:, 0]
+    z_third_back[0][HALF] = z_inverse[0]
+    z_fifth = np.zeros((3, N, N))
+    for r, count in enumerate((21, 21, 1)):
+        lanes, waves = spares(21 * r, count)
+        z_fifth[r][lanes] = z_inverse[waves]
     wave = np.arange(KEPT)
     wave = np.where(wave < BAND, wave, wave - KEPT)
     angle = turn * ((wave[:, None] * cell[None, :]) % N)
@@ -62,7 +79,18 @@
         high, low = split_np(table)
         return np.concatenate([high, high, low], axis=0)
 
-    return right(z_forward), right(z_inverse), right(z_pair), left(forward), left(inverse)
+    def beside(one, other):
+        return right(np.concatenate([one, other], axis=1))
+
+    return (
+        right(z_forward),
+        beside(z_third[0], z_third[1]),
+        left(forward),
+        left(inverse),
+        np.stack([beside(z_inverse, z_fifth[r]) for r in range(3)]),
+        np.stack([right(z_turned), right(z_inverse)]),
+        np.stack([beside(z_inverse, z_third_back[r]) for r in range(2)]),
+    )
 
 
 def halves(value):
@@ -92,8 +120,8 @@
 
 
 def kernel(
-    v_hbm, zf_hbm, zi_hbm, zp_hbm, xf_hbm, xi_hbm, o_hbm,
-    vin, zf, zi, zp, xf, xi, s0, r0, fs, fr, is6, ir6, is3, ir3, t0, q0, out, a0, acc,
+    v_hbm, zf_hbm, zt_hbm, xf_hbm, xi_hbm, zu_hbm, zw_hbm, zo_hbm, o_hbm,
+    vin, zf, zt, xf, xi, zu, zw, zo, s0, r0, fs, fr, is4, ir4, is3, ir3, t0, q0, out, a0, acc,
     load_sem, store_sem, ready_sem, row_s, row_r, fwd_s, fwd_r, inv_s, inv_r,
 ):
     row, col = lax.axis_index("row"), lax.axis_index("col")
@@ -105,7 +133,10 @@
     loads = [
         pltpu.make_async_copy(src, dst, load_sem.at[n])
         for n, (src, dst) in enumerate(
-            [(v_hbm, vin), (zf_hbm, zf), (xf_hbm, xf), (xi_hbm, xi), (zp_hbm, zp), (zi_hbm, zi)]
+            [
+                (v_hbm, vin), (zf_hbm, zf), (zt_hbm, zt), (xf_hbm, xf), (xi_hbm, xi),
+                (zu_hbm, zu), (zw_hbm, zw), (zo_hbm, zo),
+            ]
         )
     ]
     for load in loads:
@@ -244,32 +275,55 @@
         for c in range(rows):
             ref[pl.ds(c, N, stride=rows), :] = outs[c]
 
+    spare = lane % HALF >= BAND
+
     def with_curl(a):
-        cross = [
-            ky * a[2] - kz * a[1],
-            kz * a[0] - kx * a[2],
-            kx * a[1] - ky * a[0],
+        first = -turned(ky * a[2] - kz * a[1])
+        last = -turned(kx * a[1] - ky * a[0])
+        return [
+            jnp.where(spare, pltpu.roll(first, BAND, 1), a[0]),
+            jnp.where(spare, pltpu.roll(first, BAND - 21, 1), a[1]),
+            jnp.where(spare, pltpu.roll(first, 1, 1), a[2]),
+            last,
         ]
-        return list(a) + [-turned(w) for w in cross]
-
-    loads[0].wait()
-    loads[1].wait()
-    lines = times(vin[...], zf[...])
-    for n in range(24):
-        s0[:, n, :] = lines[n * 16 : (n + 1) * 16]
+
+    for load in loads[:3]:
+        load.wait()
+    third = times(vin[256:], zt[...])
+    for r in range(2):
+        lines = times(vin[r * N : (r + 1) * N], zf[...]) + part(third, r)
+        for n in range(8):
+            s0[:, r * 8 + n, :] = lines[n * 16 : (n + 1) * 16]
     for p in range(2):
-        ir6[p, pl.ds(KEPT * 6, (PAD - KEPT) * 6), :] = jnp.zeros(((PAD - KEPT) * 6, N), F32)
+        ir4[p, pl.ds(KEPT * 4, (PAD - KEPT) * 4), :] = jnp.zeros(((PAD - KEPT) * 4, N), F32)
     ir3[pl.ds(KEPT * 3, (PAD - KEPT) * 3), :] = jnp.zeros(((PAD - KEPT) * 3, N), F32)
 
     pl.semaphore_wait(barrier, 22)
     for j in range(1, 8):
         pl.semaphore_signal(ready_sem, inc=1, device_id=(row, (col + j) % 8))
     row_exchange(s0, r0, 0)
-    loads[2].wait()
-    put_forward(0, x_forward([r0[:, c * 8 : (c + 1) * 8, :].reshape(N, N) for c in range(3)]))
+    loads[3].wait()
+    rows = [r0[:, r * 8 : (r + 1) * 8, :].reshape(N, N) for r in range(2)]
+    low = jnp.where(
+        lane == 0,
+        pltpu.roll(rows[0], HALF, 1),
+        jnp.where(
+            lane % HALF < 22, pltpu.roll(rows[0], N - 42, 1), pltpu.roll(rows[1], N - 21, 1)
+        ),
+    )
+    put_forward(
+        0,
+        x_forward(
+            [
+                jnp.where(lane == HALF, 0.0, rows[0]),
+                rows[1],
+                jnp.where(lane == HALF, 0.0, low),
+            ]
+        ),
+    )
     pl.semaphore_wait(ready_sem, 7)
     send_forward(0)
-    for load in loads[3:]:
+    for load in loads[4:]:
         load.wait()
 
     @pl.when(active)
@@ -277,17 +331,18 @@
         a = spectral(0)
         for c in range(3):
             a0[c] = a[c]
-        scatter(with_curl(a), is6.at[0], 6)
-        send_inverse(is6.at[0], ir6.at[0], 0, 6)
+        scatter(with_curl(a), is4.at[0], 4)
+        send_inverse(is4.at[0], ir4.at[0], 0, 4)
 
     for p in range(2):
-        got = take_inverse(is6.at[p], ir6.at[p], p, 6)
-        both = x_inverse_pair(got)
-        grids = []
-        for c in range(6):
-            piece = part(both, c)
-            grids.append(times(jnp.concatenate([piece[:N], piece[N:]], axis=1), zp[...]))
-        u, w = grids[:3], grids[3:]
+        got = take_inverse(is4.at[p], ir4.at[p], p, 4)
+        got.append(kz * got[0] - ky * got[2])
+        lines = fold(x_inverse_pair(got), N, -1.0)
+        u, w = [], [None, times(lines[4], zw[0]), times(lines[3], zw[1])]
+        for c in range(3):
+            pair = times(lines[c], zu[c])
+            u.append(part(pair, 0))
+            w[0] = part(pair, 1) if c == 0 else w[0] + part(pair, 1)
         product = [
             u[1] * w[2] - u[2] * w[1],
             u[2] * w[0] - u[0] * w[2],
@@ -308,8 +363,8 @@
                     acc[c] = base + (0.5 * STEP) * rate
                     nxt.append(base + STEP * rate)
                     a0[c] = nxt[c]
-                scatter(with_curl(nxt), is6.at[1], 6)
-                send_inverse(is6.at[1], ir6.at[1], 1, 6)
+                scatter(with_curl(nxt), is4.at[1], 4)
+                send_inverse(is4.at[1], ir4.at[1], 1, 4)
             else:
                 last = []
                 for c in range(3):
@@ -319,14 +374,22 @@
 
     got = take_inverse(is3, ir3, 2, 3)
     ends = fold(x_inverse_pair(got), N, -1.0)
-    for c in range(3):
-        t0[:, c * 8 : (c + 1) * 8, :] = ends[c].reshape(16, 8, N)
+    packed = [
+        jnp.where(
+            lane == HALF,
+            pltpu.roll(ends[2], HALF, 1),
+            jnp.where(spare, pltpu.roll(ends[2], 42, 1), ends[0]),
+        ),
+        jnp.where(spare, pltpu.roll(ends[2], 21, 1), ends[1]),
+    ]
+    for r in range(2):
+        t0[:, r * 8 : (r + 1) * 8, :] = packed[r].reshape(16, 8, N)
     row_exchange(t0, q0, 1)
-    final = times(q0[...].reshape(384, N), zi[...])
+    pairs = [times(q0[:, r * 8 : (r + 1) * 8, :].reshape(N, N), zo[r]) for r in range(2)]
+    final = [part(pairs[0], 0), part(pairs[1], 0), part(pairs[0], 1) + part(pairs[1], 1)]
     for y in range(16):
         for c in range(3):
-            at = y * 24 + c * 8
-            out[pl.ds(c * 128 + y, 8, stride=16), :] = final[at : at + 8]
+            out[pl.ds(c * 128 + y, 8, stride=16), :] = final[c][y * 8 : y * 8 + 8]
     store = pltpu.make_async_copy(out, o_hbm, store_sem)
     store.start()
 
@@ -337,7 +400,7 @@
         def _():
             wait_rows(fs.at[p], (KEPT - 1) * 3, fwd_s.at[p])
             if p < 2:
-                wait_rows(is6.at[p], 127 * 6, inv_s.at[p])
+                wait_rows(is4.at[p], 127 * 4, inv_s.at[p])
             else:
                 wait_rows(is3, 127 * 3, inv_s.at[p])
 
@@ -353,13 +416,13 @@
     shapes = [((384, N), F32)] + [(t.shape, BF16) for t in consts]
     scratch = [VMEM(shape, kind) for shape, kind in shapes]
     scratch += [
-        VMEM((16, 24, N), F32), VMEM((16, 24, N), F32),
+        VMEM((16, 16, N), F32), VMEM((16, 16, N), F32),
         VMEM((3, PAD * 3, N), F32), VMEM((3, N * 3, N), F32),
-        VMEM((2, N * 6, N), F32), VMEM((2, PAD * 6, N), F32),
+        VMEM((2, N * 4, N), F32), VMEM((2, PAD * 4, N), F32),
         VMEM((N * 3, N), F32), VMEM((PAD * 3, N), F32),
-        VMEM((16, 24, N), F32), VMEM((16, 24, N), F32),
+        VMEM((16, 16, N), F32), VMEM((16, 16, N), F32),
         VMEM((384, N), F32), VMEM((3, PAD, N), F32), VMEM((3, PAD, N), F32),
-        pltpu.SemaphoreType.DMA((6,)), pltpu.SemaphoreType.DMA(()),
+        pltpu.SemaphoreType.DMA((8,)), pltpu.SemaphoreType.DMA(()),
         pltpu.SemaphoreType.REGULAR,
         pltpu.SemaphoreType.DMA((2,)), pltpu.SemaphoreType.DMA((2,)),
         pltpu.SemaphoreType.DMA((3,)), pltpu.SemaphoreType.DMA((3,)),
@@ -369,7 +432,7 @@
     result = pl.pallas_call(
         kernel,
         out_shape=jax.ShapeDtypeStruct((384, N), F32),
-        in_specs=[anywhere] * 6,
+        in_specs=[anywhere] * 8,
         out_specs=anywhere,
         scratch_shapes=scratch,
         compiler_params=pltpu.CompilerParams(collective_id=0, has_side_effects=True),

time: 67.1 us -> 64.4 us (0.960)
  Pallas kernels: 65.4 us -> 62.6 us
    pallas_call x1, Pallas kernels: 65.4 us -> 62.6 us  [local(): pl.pallas_call(kernel, out_shape=jax.ShapeDtypeStruct((384, N), F32), in_...]
where the time goes in v2:
time: 64.4 us; the launch traced here: 64.2 us
  Pallas kernels  62.6 us (97%)
  local copies, waits for them, and re-layouts  1.62 us (3%)
    pallas_call x1, Pallas kernels, local(): pl.pallas_call(kernel, out_shape=jax.ShapeDtypeStruct((384, N), F32), in_...  62.6 us
    unnamed x1, local copies, waits for them, and re-layouts  1.62 us

profile of v2, /device:TPU:1, one launch (start us, length us, event | category | flops | bytes accessed | tf_op | source)
XLA Modules:
  0.0 64.2 jit_solution(16838438373110581946)
XLA Ops:
  0.0 62.6 %heun.1 = f32[384,128]{1,0:T(8,128)} custom-call(f32[384,128]{1,0:T(8,128)} %bitcast.3, bf16[384,128]{1,0:T(8,128)(2,1)} %constant.14.clone.zf_hbm, bf16[384,256]{1,0:T(8,128)(2,1)} %constant.15.clone.zt_hbm, bf16[192,384]{1,0:T(8,128)(2,1)} %constant.16.clone.xf_hbm, bf16[256,288]{1,0:T(8,128)(2,1)} %constant.17.clone.xi_hbm, ...), custom_call_target="tpu_custom_call" | custom-call | tf_op jit(solution)/shard_map/heun/pallas_call | solution.py:432
  62.6 1.6 %copy.10 = f32[3,8,16,128]{3,2,1,0:T(8,128)} copy(f32[3,8,16,128]{3,2,1,0:T(8,128)} %bitcast.2) | data formatting | bytes 393216

commit v3 on v2

--- a/solution.py
+++ b/solution.py
@@ -14,6 +14,7 @@
 PAD = 96
 HALF = 64
 F32 = jnp.float32
+SPARE_AT = 0
 BF16 = jnp.bfloat16
 VMEM = pltpu.VMEM
 STEP = 2.0 / N
@@ -204,17 +205,25 @@
                 fwd_s.at[p], fwd_r.at[p], device_id=to,
             ).start()
 
-        for move in MOVES:
+        own = (row // 2) * 8 + col
+        first = (own // 3) % (KEPT - 64)
+
+        def to_spare(turn):
+            n = (first + turn) % (KEPT - 64)
+            chip = n * 3
+            one(64 + n, ((chip // 8) * 2, chip % 8))
+
+        for at, move in enumerate(MOVES):
+            if at == SPARE_AT:
+                @pl.when(ki != 64 + first)
+                def _():
+                    to_spare(0)
+
+                for turn in range(1, KEPT - 64):
+                    to_spare(turn)
             base, side_col = chip_at(move)
             chip = (base // 2) * 8 + side_col
-            spare = (chip % 3 == 0) & (chip < 63)
-            near = move == (0, 0, 0)
-
-            @pl.when(spare & (core == 1) if near else spare)
-            def _():
-                one(64 + chip // 3, (base, side_col))
-
-            if near:
+            if move == (0, 0, 0):
                 @pl.when(core == 0)
                 def _():
                     one(chip, (base + 1, side_col))

time: 64.4 us -> 63.7 us (0.989)
    pallas_call x1, Pallas kernels: 62.6 us -> 62 us  [local(): pl.pallas_call(kernel, out_shape=jax.ShapeDtypeStruct((384, N), F32), in_...]
where the time goes in v3:
time: 63.7 us; the launch traced here: 63.6 us
  Pallas kernels  62 us (97%)
  local copies, waits for them, and re-layouts  1.62 us (3%)
    pallas_call x1, Pallas kernels, local(): pl.pallas_call(kernel, out_shape=jax.ShapeDtypeStruct((384, N), F32), in_...  62 us
    unnamed x1, local copies, waits for them, and re-layouts  1.62 us

profile of v3, /device:TPU:1, one launch (start us, length us, event | category | flops | bytes accessed | tf_op | source)
XLA Modules:
  0.0 63.6 jit_solution(3835175385595985826)
XLA Ops:
  0.0 62.0 %heun.1 = f32[384,128]{1,0:T(8,128)} custom-call(f32[384,128]{1,0:T(8,128)} %bitcast.3, bf16[384,128]{1,0:T(8,128)(2,1)} %constant.14.clone.zf_hbm, bf16[384,256]{1,0:T(8,128)(2,1)} %constant.15.clone.zt_hbm, bf16[192,384]{1,0:T(8,128)(2,1)} %constant.16.clone.xf_hbm, bf16[256,288]{1,0:T(8,128)(2,1)} %constant.17.clone.xi_hbm, ...), custom_call_target="tpu_custom_call" | custom-call | tf_op jit(solution)/shard_map/heun/pallas_call | solution.py:441
  62.0 1.6 %copy.10 = f32[3,8,16,128]{3,2,1,0:T(8,128)} copy(f32[3,8,16,128]{3,2,1,0:T(8,128)} %bitcast.2) | data formatting | bytes 393216

commit v4 on v3

--- a/solution.py
+++ b/solution.py
@@ -20,6 +20,10 @@
 STEP = 2.0 / N
 MOVES = sorted(
     itertools.product(range(4), repeat=3), key=lambda move: -sum((0, 1, 2, 1)[d] for d in move)
+)
+TARGETS = sorted(
+    itertools.product(MOVES[:-1], range(2)),
+    key=lambda to: -sum((0, 1, 2, 1)[d] for d in to[0]) - 0.6 * (1 - to[1]),
 )
 ROW_MOVES = [move for move in itertools.product(range(4), range(2), range(2)) if any(move)]
 ROW_MOVES.sort(key=lambda move: -((0, 1, 2, 1)[move[0]] + 2 * move[1]))
@@ -247,11 +251,10 @@
                 inv_s.at[p], inv_r.at[p], device_id=to,
             ).start()
 
-        for move in MOVES:
+        for move, to_core in TARGETS:
             base, side_col = chip_at(move)
-            for other in range(2):
-                if move != (0, 0, 0) or other:
-                    one((base + (core + other) % 2, side_col))
+            one((base + to_core, side_col))
+        one((row + 1 - 2 * core, col))
 
     def take_inverse(src, dst, p, rows):
         @pl.when(active)

time: 63.7 us -> 63.1 us (level)
  Pallas kernels: 62 us -> 61.3 us
    pallas_call x1, Pallas kernels: 62 us -> 61.3 us  [local(): pl.pallas_call(kernel, out_shape=jax.ShapeDtypeStruct((384, N), F32), in_...]
where the time goes in v4:
time: 63.1 us; the launch traced here: 62.9 us
  Pallas kernels  61.3 us (97%)
  local copies, waits for them, and re-layouts  1.62 us (3%)
    pallas_call x1, Pallas kernels, local(): pl.pallas_call(kernel, out_shape=jax.ShapeDtypeStruct((384, N), F32), in_...  61.3 us
    unnamed x1, local copies, waits for them, and re-layouts  1.62 us

profile of v4, /device:TPU:1, one launch (start us, length us, event | category | flops | bytes accessed | tf_op | source)
XLA Modules:
  0.0 62.9 jit_solution(3731456923660112614)
XLA Ops:
  0.0 61.3 %heun.1 = f32[384,128]{1,0:T(8,128)} custom-call(f32[384,128]{1,0:T(8,128)} %bitcast.3, bf16[384,128]{1,0:T(8,128)(2,1)} %constant.14.clone.zf_hbm, bf16[384,256]{1,0:T(8,128)(2,1)} %constant.15.clone.zt_hbm, bf16[192,384]{1,0:T(8,128)(2,1)} %constant.16.clone.xf_hbm, bf16[256,288]{1,0:T(8,128)(2,1)} %constant.17.clone.xi_hbm, ...), custom_call_target="tpu_custom_call" | custom-call | tf_op jit(solution)/shard_map/heun/pallas_call | solution.py:444
  61.3 1.6 %copy.10 = f32[3,8,16,128]{3,2,1,0:T(8,128)} copy(f32[3,8,16,128]{3,2,1,0:T(8,128)} %bitcast.2) | data formatting | bytes 393216
